TPU v7x, 32 devices: a whole 2x2x4 slice. The times are simulated.
32 devices in a mesh: dp: 8 (over z, x), mp: 4 (over y, core).
Axes of the slice: x: 2, y: 2, z: 4, core: 2. Of those that a mesh axis runs over, the one named last changes fastest.
Arguments:
- hidden: bfloat16 [8, 512, 4608], P('dp', 'mp'), may hold values from -6 to 6
- lengths: int32 [8], P('dp'), may hold values from 64 to 512
- norm_gain: float32 [4608], replicated, may hold values from 0.25 to 1.75
- w_query: bfloat16 [4608, 2048], P('dp', 'mp'), may hold values from -0.09375 to 0.09375
- w_key: bfloat16 [4608, 1024], P('dp', 'mp'), may hold values from -0.09375 to 0.09375
- w_value: bfloat16 [4608, 1024], P('dp', 'mp'), may hold values from -0.09375 to 0.09375
- w_out: bfloat16 [2048, 4608], P('mp', 'dp'), may hold values from -0.125 to 0.125
- post_gain: float32 [4608], replicated, may hold values from 0.25 to 1.75
Outputs:
- mixed: bfloat16 [8, 512, 4608], P('dp', 'mp')
- key_cache: bfloat16 [8, 512, 1024], P('dp', None, 'mp')
- value_cache: bfloat16 [8, 512, 1024], P('dp', None, 'mp')
All inputs are finite; a program needn't handle non-finite values.
Results may differ from a plain program's by a relative error of at most 0.01.
Values may be sent and summed in bfloat16 or wider, within the bound.
A program may use at most 128 MiB of HBM per device.

v0:
```python
import functools

import jax
import jax.numpy as jnp
import numpy as np
from jax import lax
from jax.experimental import pallas as pl
from jax.experimental.pallas import tpu as pltpu
from jax.sharding import PartitionSpec as P

HD = 128
MESH = pl.DeviceIdType.MESH
UP, DOWN, ACROSS = 0, 1, 2


def tables(maxlen):
    half = HD // 2
    freqs = 10000.0 ** (-np.arange(half, dtype=np.float64) / half)
    angles = np.arange(maxlen, dtype=np.float64)[:, None] * freqs[None, :]
    cosine, sine = np.cos(angles), np.sin(angles)
    return (
        np.concatenate([cosine, cosine], axis=1).astype(np.float32),
        np.concatenate([-sine, sine], axis=1).astype(np.float32),
    )


def cut(rows):
    if rows % 32:
        return [None, (0, rows)]
    first = rows // 6 // 16 * 16
    rest = rows - first
    chunk = rest // 2 // 16 * 16
    return [(0, first), (first, chunk), (first + chunk, rest - chunk)]


def kernel(
    n_dp, n_mp, cuts,
    len_ref, hid, ngain, wq, wk, wv, wo, pgain, cos_ref, sin_ref,
    mixed, key_out, val_out,
    wbuf, obuf, nbuf, acc, att, psend, precv, inbox,
    load_sem, send_sem, recv_sem, nsend_sem, nrecv_sem, psend_sem, precv_sem, fsend_sem, inbox_sem,
):
    nz = n_dp // 2
    me, mp = lax.axis_index("dp"), lax.axis_index("mp")
    z, x = me // 2, me % 2
    local_len, width = hid.shape
    maxlen = local_len * n_mp
    fcols = width // n_dp
    qw, kw = wq.shape[1], wk.shape[1]
    q_heads, kv_heads = qw // HD, kw // HD
    can_up, can_down = z < nz - 1, z > 0
    bufs = (wbuf, obuf)

    loads = [
        pltpu.make_async_copy(wq, wbuf.at[me, :, pl.ds(0, qw)], load_sem.at[0]),
        pltpu.make_async_copy(wk, wbuf.at[me, :, pl.ds(qw, kw)], load_sem.at[1]),
        pltpu.make_async_copy(wv, wbuf.at[me, :, pl.ds(qw + kw, kw)], load_sem.at[2]),
        pltpu.make_async_copy(wo, obuf.at[me], load_sem.at[3]),
    ]
    for load in loads:
        load.start()

    barrier = pltpu.get_barrier_semaphore()

    def greet(dp_index, mp_index):
        pl.semaphore_signal(barrier, inc=1, device_id=(dp_index, mp_index), device_id_type=MESH)

    greet(me + 1 - 2 * x, mp)
    for step in range(1, n_mp):
        greet(me, lax.rem(mp + step, n_mp))

    @pl.when(can_up)
    def _():
        greet(me + 2, mp)

    @pl.when(can_down)
    def _():
        greet(me - 2, mp)

    pl.semaphore_wait(
        barrier, n_mp + jnp.where(can_up, 1, 0) + jnp.where(can_down, 1, 0)
    )

    def copy(kind, part, origin, way):
        start, size = cuts[kind][part]
        ref = bufs[kind].at[origin, pl.ds(start, size)]
        target = (me + 2, me - 2, me + 1 - 2 * x)[way]
        return pltpu.make_async_remote_copy(
            src_ref=ref,
            dst_ref=ref,
            send_sem=send_sem.at[kind, part, way, origin],
            recv_sem=recv_sem.at[kind, part, origin],
            device_id=(target, mp),
            device_id_type=MESH,
        )

    def send_chain(kind, part, origin):
        @pl.when(can_up)
        def _():
            copy(kind, part, origin, UP).start()

        @pl.when(can_down)
        def _():
            copy(kind, part, origin, DOWN).start()

    def rest_of(kind):
        return range(1, len(cuts[kind]))

    def send_own(kind):
        if cuts[kind][0]:
            copy(kind, 0, me, ACROSS).start()
        for part in rest_of(kind):
            send_chain(kind, part, me)
            copy(kind, part, me, ACROSS).start()
        if cuts[kind][0]:
            send_chain(kind, 0, me)

    def send_partner(kind):
        if cuts[kind][0]:
            partner = me + 1 - 2 * x
            copy(kind, 0, partner, ACROSS).wait_recv()
            send_chain(kind, 0, partner)

    def relay(kind, k):
        below, above = z - k, z + k
        for part in rest_of(kind):
            @pl.when(below >= 0)
            def _():
                origin = below * 2 + x
                copy(kind, part, origin, UP).wait_recv()

                @pl.when(can_up)
                def _():
                    copy(kind, part, origin, UP).start()

                copy(kind, part, origin, ACROSS).start()

            @pl.when(above < nz)
            def _():
                origin = above * 2 + x
                copy(kind, part, origin, DOWN).wait_recv()

                @pl.when(can_down)
                def _():
                    copy(kind, part, origin, DOWN).start()

                copy(kind, part, origin, ACROSS).start()

        if cuts[kind][0]:
            for column in range(2):
                @pl.when(below >= 0)
                def _():
                    origin = below * 2 + column
                    copy(kind, 0, origin, UP).wait_recv()

                    @pl.when(can_up)
                    def _():
                        copy(kind, 0, origin, UP).start()

                @pl.when(above < nz)
                def _():
                    origin = above * 2 + column
                    copy(kind, 0, origin, DOWN).wait_recv()

                    @pl.when(can_down)
                    def _():
                        copy(kind, 0, origin, DOWN).start()

    def wait_across(kind, origin):
        for part in rest_of(kind):
            copy(kind, part, origin, ACROSS).wait_recv()

    def drain(kind):
        def body(origin, carry):
            oz, ox = origin // 2, origin % 2
            for part in range(len(cuts[kind])):
                if not cuts[kind][part]:
                    continue
                mine = (ox == x) | (part == 0)

                @pl.when(mine & (oz <= z) & can_up)
                def _():
                    copy(kind, part, origin, UP).wait_send()

                @pl.when(mine & (oz >= z) & can_down)
                def _():
                    copy(kind, part, origin, DOWN).wait_send()

                @pl.when((origin == me) if part == 0 else (ox == x))
                def _():
                    copy(kind, part, origin, ACROSS).wait_send()

            return carry

        lax.fori_loop(0, n_dp, body, 0)

    for load in loads[:3]:
        load.wait()
    send_own(0)

    total = jnp.zeros((local_len, 1), jnp.float32)
    for block in range(n_dp):
        rows = hid[:, block * fcols : (block + 1) * fcols].astype(jnp.float32)
        total = total + jnp.sum(rows * rows, axis=-1, keepdims=True)
    scale = lax.rsqrt(total / width + 1e-06)
    for block in range(n_dp):
        span = slice(block * fcols, (block + 1) * fcols)
        rows = hid[:, span].astype(jnp.float32)
        nbuf[mp, block] = (rows * scale * ngain[:, span]).astype(jnp.bfloat16)

    def share(step):
        return pltpu.make_async_remote_copy(
            src_ref=nbuf.at[mp],
            dst_ref=nbuf.at[mp],
            send_sem=nsend_sem.at[step],
            recv_sem=nrecv_sem.at[mp],
            device_id=(me, lax.rem(mp + step, n_mp)),
            device_id_type=MESH,
        )

    def shared(source):
        return pltpu.make_async_remote_copy(
            src_ref=nbuf.at[source],
            dst_ref=nbuf.at[source],
            send_sem=nsend_sem.at[0],
            recv_sem=nrecv_sem.at[source],
            device_id=(me, source),
            device_id_type=MESH,
        )

    for step in range(1, n_mp):
        share(step).start()
    send_partner(0)
    acc[...] = jnp.zeros_like(acc)

    def step_qkv(k, carry):
        relay(0, k)
        return carry

    lax.fori_loop(1, nz, step_qkv, 0)
    loads[3].wait()
    send_own(1)
    for step in range(1, n_mp):
        shared(lax.rem(mp + step, n_mp)).wait_recv()

    def project(i, carry):
        other, k, side = i // (2 * nz), i // 2 % nz, i % 2
        oz = z + k * (2 * side - 1)
        origin = oz * 2 + lax.rem(x + other, 2)

        @pl.when((oz >= 0) & (oz < nz) & ((side == 0) | (k > 0)))
        def _():
            @pl.when(other == 1)
            def _():
                wait_across(0, origin)

            for m in range(n_mp):
                span = slice(m * local_len, (m + 1) * local_len)
                acc[span, :] += jnp.dot(
                    nbuf[m, origin], wbuf[origin], preferred_element_type=jnp.float32
                )

        return carry

    lax.fori_loop(0, 4 * nz, project, 0)
    send_partner(1)

    length = len_ref[0]
    live = lax.broadcasted_iota(jnp.int32, (maxlen, HD), 0) < length

    def rotated(block, span):
        return block * cos_ref[span, :] + pltpu.roll(block, HD // 2, 1) * sin_ref[span, :]

    everything = slice(0, maxlen)
    for h in range(kv_heads):
        cols = slice(h * HD, (h + 1) * HD)
        keys = rotated(acc[:, qw + h * HD : qw + (h + 1) * HD], everything)
        key_out[:, cols] = jnp.where(live, keys, 0.0).astype(jnp.bfloat16)
        values = acc[:, qw + kw + h * HD : qw + kw + (h + 1) * HD]
        val_out[:, cols] = jnp.where(live, values, 0.0).astype(jnp.bfloat16)
    for h in range(q_heads):
        kv = h * kv_heads // q_heads
        cols = slice(kv * HD, (kv + 1) * HD)
        for r in range(n_mp):
            span, seen = slice(r * local_len, (r + 1) * local_len), (r + 1) * local_len
            query = rotated(acc[span, h * HD : (h + 1) * HD], span) * 144.0 ** (-0.5)
            score = lax.dot_general(
                query.astype(jnp.bfloat16),
                key_out[:seen, cols],
                (((1,), (1,)), ((), ())),
                preferred_element_type=jnp.float32,
            )
            row = lax.broadcasted_iota(jnp.int32, score.shape, 0) + r * local_len
            col = lax.broadcasted_iota(jnp.int32, score.shape, 1)
            expo = jnp.exp(50.0 * jnp.tanh(score * (1.0 / 50.0)))
            expo = jnp.where((col <= row) & (col < length), expo, 0.0)
            weights = (expo / jnp.sum(expo, axis=-1, keepdims=True)).astype(jnp.bfloat16)
            att[span, h * HD : (h + 1) * HD] = jnp.dot(
                weights, val_out[:seen, cols], preferred_element_type=jnp.float32
            ).astype(jnp.bfloat16)

    pairs = n_mp // 2
    mate = mp + 1 - 2 * lax.rem(mp, 2)

    def hand(block, step):
        part = lax.rem(mate + 2 * step, n_mp)
        return pltpu.make_async_remote_copy(
            src_ref=psend.at[block, part],
            dst_ref=precv.at[block, 0] if step == 0 else inbox.at[block, step - 1],
            send_sem=psend_sem.at[block, step],
            recv_sem=precv_sem.at[block, 0] if step == 0 else inbox_sem.at[block, step - 1],
            device_id=(me, mate),
            device_id_type=MESH,
        )

    def far(block, step):
        target = lax.rem(mp + 2 * step, n_mp)
        return pltpu.make_async_remote_copy(
            src_ref=psend.at[block, target],
            dst_ref=precv.at[block, pairs - step],
            send_sem=fsend_sem.at[block, step - 1],
            recv_sem=precv_sem.at[block, pairs - step],
            device_id=(me, target),
            device_id_type=MESH,
        )

    def forward(block):
        for step in range(1, pairs):
            hand(block, step).wait_recv()
            target = lax.rem(mp + 2 * step, n_mp)
            both = psend[block, target].astype(jnp.float32) + inbox[block, step - 1].astype(
                jnp.float32
            )
            psend[block, target] = both.astype(jnp.bfloat16)
            far(block, step).start()

    def output(block):
        for m in range(n_mp):
            span = slice(m * local_len, (m + 1) * local_len)
            psend[block, m] = jnp.dot(
                att[span, :], obuf[block], preferred_element_type=jnp.float32
            ).astype(jnp.bfloat16)
        for step in list(range(1, pairs)) + [0]:
            hand(block, step).start()

    def step_out(k, carry):
        @pl.when((k > 0) & (k < nz))
        def _():
            relay(1, k)

        def each(i, inner):
            other, side = i // 2, i % 2
            distance = k - other
            oz = z + distance * (2 * side - 1)
            origin = oz * 2 + lax.rem(x + other, 2)

            @pl.when(
                (distance >= 0) & (distance < nz) & (oz >= 0) & (oz < nz)
                & ((side == 0) | (distance > 0))
            )
            def _():
                @pl.when(other == 1)
                def _():
                    wait_across(1, origin)

                output(origin)
                forward(origin)

            return inner

        return lax.fori_loop(0, 4, each, carry)

    lax.fori_loop(0, nz + 1, step_out, 0)

    def summed(block):
        value = psend[block, mp].astype(jnp.float32)
        for slot in range(pairs):
            value = value + precv[block, slot].astype(jnp.float32)
        return value

    def squares(block, total):
        hand(block, 0).wait_recv()
        for step in range(1, pairs):
            far(block, step).wait_recv()
        value = summed(block)
        return total + jnp.sum(value * value, axis=-1, keepdims=True)

    total = lax.fori_loop(0, n_dp, squares, jnp.zeros((local_len, 1), jnp.float32))
    scale = lax.rsqrt(total / width + 1e-06)
    own = lax.broadcasted_iota(jnp.int32, (local_len, fcols), 0) + mp * local_len < length
    for block in range(n_dp):
        span = slice(block * fcols, (block + 1) * fcols)
        post = summed(block) * scale * pgain[:, span]
        mixed[:, span] = jnp.where(own, hid[:, span].astype(jnp.float32) + post, 0.0).astype(
            jnp.bfloat16
        )

    drain(0)
    drain(1)
    for step in range(1, n_mp):
        share(step).wait_send()

    def drain_hand(block, carry):
        for step in range(pairs):
            hand(block, step).wait_send()
        for step in range(1, pairs):
            far(block, step).wait_send()
        return carry

    lax.fori_loop(0, n_dp, drain_hand, 0)


def local(n_dp, n_mp, hidden, lengths, norm_gain, w_query, w_key, w_value, w_out, post_gain):
    _, local_len, width = hidden.shape
    maxlen = local_len * n_mp
    rows, qw = w_query.shape
    kw = w_key.shape[1]
    orows, fcols = w_out.shape
    cuts = (cut(rows), cut(orows))
    cosine, sine = tables(maxlen)
    vmem = pl.BlockSpec(memory_space=pltpu.VMEM)
    anywhere = pl.BlockSpec(memory_space=pl.ANY)
    bf16, f32 = jnp.bfloat16, jnp.float32
    dma = pltpu.SemaphoreType.DMA
    mixed, keys, values = pl.pallas_call(
        functools.partial(kernel, n_dp, n_mp, cuts),
        out_shape=(
            jax.ShapeDtypeStruct((local_len, width), bf16),
            jax.ShapeDtypeStruct((maxlen, kw), bf16),
            jax.ShapeDtypeStruct((maxlen, kw), bf16),
        ),
        in_specs=[pl.BlockSpec(memory_space=pltpu.SMEM), vmem, vmem]
        + [anywhere] * 4
        + [vmem, vmem, vmem],
        out_specs=(vmem, vmem, vmem),
        scratch_shapes=[
            pltpu.VMEM((n_dp, rows, qw + 2 * kw), bf16),
            pltpu.VMEM((n_dp, orows, fcols), bf16),
            pltpu.VMEM((n_mp, n_dp, local_len, fcols), bf16),
            pltpu.VMEM((maxlen, qw + 2 * kw), f32),
            pltpu.VMEM((maxlen, qw), bf16),
            pltpu.VMEM((n_dp, n_mp, local_len, fcols), bf16),
            pltpu.VMEM((n_dp, n_mp // 2, local_len, fcols), bf16),
            pltpu.VMEM((n_dp, n_mp // 2 - 1, local_len, fcols), bf16),
            dma((4,)),
            dma((2, 3, 3, n_dp)),
            dma((2, 3, n_dp)),
            dma((n_mp,)),
            dma((n_mp,)),
            dma((n_dp, n_mp // 2)),
            dma((n_dp, n_mp // 2)),
            dma((n_dp, n_mp // 2 - 1)),
            dma((n_dp, n_mp // 2 - 1)),
        ],
        compiler_params=pltpu.CompilerParams(
            collective_id=0, has_side_effects=True, vmem_limit_bytes=60 * 1024 * 1024
        ),
    )(
        lengths,
        hidden[0],
        norm_gain.reshape(1, width),
        w_query,
        w_key,
        w_value,
        w_out,
        post_gain.reshape(1, width),
        jnp.asarray(cosine),
        jnp.asarray(sine),
    )
    return mixed[None], keys[None], values[None]


def solution(mesh):
    return jax.shard_map(
        functools.partial(local, mesh.shape["dp"], mesh.shape["mp"]),
        mesh=mesh,
        in_specs=(
            P("dp", "mp", None),
            P("dp"),
            P(),
            P("dp", "mp"),
            P("dp", "mp"),
            P("dp", "mp"),
            P("mp", "dp"),
            P(),
        ),
        out_specs=(P("dp", "mp", None), P("dp", None, "mp"), P("dp", None, "mp")),
        check_vma=False,
    )
```

profile of v0, /device:TPU:0, one launch (start us, length us, event | category | flops | bytes accessed | tf_op | source)
XLA Modules:
  0.0 172.6 jit_solution(8630637121706815162)
XLA Ops:
  1.3 1.3 reshape.12.ngain
  2.6 1.3 reshape.13.pgain
  4.0 2.1 %copy.13.wo = bf16[512,576]{1,0:T(8,128)(2,1)} copy(bf16[512,576]{0,1:T(8,128)(2,1)} %param.16) | data formatting | bytes 1179648 | tf_op args[6]
  6.1 162.6 %shard_map.121 = (bf16[128,4608]{1,0:T(8,128)(2,1)}, bf16[512,256]{1,0:T(8,128)(2,1)}, bf16[512,256]{1,0:T(8,128)(2,1)}) custom-call(s32[1]{0:T(128)S(6)} %copy.17.len_ref, bf16[128,4608]{1,0:T(8,128)(2,1)} %bitcast.4, f32[1,4608]{1,0:T(1,128)} %reshape.12.ngain, bf16[576,512]{1,0:T(8,128)(2,1)} %wq.1, bf16[576,256]{1,0:T(8,128)(2,1)} %wk.1, ...), custom_call_target="tpu_custom_call" | custom-call | tf_op jit(solution)/shard_map/pallas_call | solution.py:425
  168.7 0.0 copy-start.1
  168.7 0.0 copy-start
  168.7 2.4 %copy.18 = bf16[1,128,4608]{2,1,0:T(8,128)(2,1)} copy(bf16[1,128,4608]{2,1,0:T(8,128)(2,1)} %bitcast.5) | data formatting | bytes 2359296
  171.2 0.0 copy-done.1
  171.2 0.7 copy.19
  171.9 0.0 copy-done
  171.9 0.7 copy.20
Async XLA Ops:
  168.7 2.4 %copy-start.1 = (bf16[512,256]{1,0:T(8,128)(2,1)S(1)}, bf16[512,256]{1,0:T(8,128)(2,1)}, u32[]{:S(2)}) copy-start(bf16[512,256]{1,0:T(8,128)(2,1)} %get-tuple-element.7) | copy-start | bytes 786436
  168.7 3.1 %copy-start = (bf16[512,256]{1,0:T(8,128)(2,1)S(1)}, bf16[512,256]{1,0:T(8,128)(2,1)}, u32[]{:S(2)}) copy-start(bf16[512,256]{1,0:T(8,128)(2,1)} %get-tuple-element.8) | copy-start | bytes 786436
where the time goes:
time: 173 us
  Pallas kernels  163 us (94%)
  local copies, waits for them, and re-layouts  8.66 us (5%)
    pallas_call x1, Pallas kernels, local(): pl.pallas_call(functools.partial(kernel, n_dp, n_mp, cuts), out_shape=(ja...  163 us
    unnamed x8, local copies, waits for them, and re-layouts  5.97 us

commit v1 on v0

v1 whole, which is shorter than its diff:
```python
import functools

import jax
import jax.numpy as jnp
import numpy as np
from jax import lax
from jax.experimental import pallas as pl
from jax.experimental.pallas import tpu as pltpu
from jax.sharding import PartitionSpec as P

HD = 128
LANES = 128
MESH = pl.DeviceIdType.MESH
UP, DOWN = 0, 1
OWN, OTHER = 0, 1


def tables(maxlen):
    half = HD // 2
    freqs = 10000.0 ** (-np.arange(half, dtype=np.float64) / half)
    angles = np.arange(maxlen, dtype=np.float64)[:, None] * freqs[None, :]
    cosine, sine = np.cos(angles), np.sin(angles)
    return (
        np.concatenate([cosine, cosine], axis=1).astype(np.float32),
        np.concatenate([-sine, sine], axis=1).astype(np.float32),
    )


def cut(rows):
    pieces, start = [], 0
    while start < rows:
        size = min(256, rows - start)
        pieces.append((start, size))
        start += size
    return pieces


def kernel(
    n_dp, n_mp, pieces,
    len_ref, hid_in, ngain_in, wq, wk, wv, wo, pgain_in, cos_in, sin_in,
    mixed, key_out, val_out,
    *scratch,
):
    ns = len(pieces)
    (
        hid, ngain_t, pgain_t, ngain, pgain, cos_ref, sin_ref,
        wbuf, obuf, nbuf, acc, pout, pin, kbuf, vbuf, vext, att, sq, mbuf,
    ) = scratch[:19]
    rest = scratch[19:]
    psend, inbox, precv, xout, yall = (rest[i * ns : (i + 1) * ns] for i in range(5))
    (
        load_sem, zsend, zrecv, xsend, xmate, xfar, xrecv, qsend, qrecv, asend, arecv,
        hsend, hrecv, fsend, frecv, csend, crecv, osem,
    ) = rest[5 * ns :]

    nz = n_dp // 2
    pairs = n_mp // 2
    me, mp = lax.axis_index("dp"), lax.axis_index("mp")
    z, x = me // 2, me % 2
    side, slot = mp % 2, mp // 2
    partner = me + 1 - 2 * x
    mate = mp + 1 - 2 * side
    local_len, width = hid.shape
    maxlen = local_len * n_mp
    fcols = width // n_dp
    qw, kw = wq.shape[1], wk.shape[1]
    nq = qw // kw
    nc = 2 + nq
    q_heads, kv_heads = qw // HD, kw // HD
    can_up, can_down = z < nz - 1, z > 0
    middle = can_up & can_down
    f32, bf16 = jnp.float32, jnp.bfloat16

    def remote(src, dst, send, recv, dp_index, mp_index):
        return pltpu.make_async_remote_copy(
            src_ref=src, dst_ref=dst, send_sem=send, recv_sem=recv,
            device_id=(dp_index, mp_index), device_id_type=MESH,
        )

    load_w = [
        pltpu.make_async_copy(wk, wbuf.at[z, 0], load_sem.at[0]),
        pltpu.make_async_copy(wv, wbuf.at[z, 1], load_sem.at[1]),
    ] + [
        pltpu.make_async_copy(wq.at[:, pl.ds(j * kw, kw)], wbuf.at[z, 2 + j], load_sem.at[2 + j])
        for j in range(nq)
    ]
    load_o = pltpu.make_async_copy(wo, obuf.at[z], load_sem.at[nc])
    load_x = [
        pltpu.make_async_copy(hid_in, hid, load_sem.at[nc + 1]),
        pltpu.make_async_copy(ngain_in, ngain_t, load_sem.at[nc + 2]),
    ]
    load_r = [
        pltpu.make_async_copy(pgain_in, pgain_t, load_sem.at[nc + 3]),
        pltpu.make_async_copy(cos_in, cos_ref, load_sem.at[nc + 4]),
        pltpu.make_async_copy(sin_in, sin_ref, load_sem.at[nc + 5]),
    ]
    for load in load_w[:1] + load_x + load_w[1:] + [load_o] + load_r:
        load.start()

    barrier = pltpu.get_barrier_semaphore()

    def greet(dp_index, mp_index):
        pl.semaphore_signal(barrier, inc=1, device_id=(dp_index, mp_index), device_id_type=MESH)

    greet(partner, mp)
    for step in range(1, n_mp):
        greet(me, lax.rem(mp + step, n_mp))

    @pl.when(can_up)
    def _():
        greet(me + 2, mp)

    @pl.when(can_down)
    def _():
        greet(me - 2, mp)

    pl.semaphore_wait(
        barrier, n_mp + jnp.where(can_up, 1, 0) + jnp.where(can_down, 1, 0)
    )

    def item(c, origin):
        if c < nc:
            return wbuf.at[origin, c]
        start, size = pieces[c - nc]
        return obuf.at[origin, pl.ds(start, size)]

    def copy(c, origin, way):
        ref = item(c, origin)
        return remote(
            ref, ref, zsend.at[c, way, origin], zrecv.at[c, origin],
            (me + 2, me - 2)[way], mp,
        )

    def send_own(c):
        @pl.when(can_up)
        def _():
            copy(c, z, UP).start()

        @pl.when(can_down)
        def _():
            copy(c, z, DOWN).start()

    def relay(c, k):
        below, above = z - k, z + k

        @pl.when(below >= 0)
        def _():
            copy(c, below, UP).wait_recv()

            @pl.when(can_up)
            def _():
                copy(c, below, UP).start()

        @pl.when(above < nz)
        def _():
            copy(c, above, DOWN).wait_recv()

            @pl.when(can_down)
            def _():
                copy(c, above, DOWN).start()

    def relays(c, first, last):
        def body(k, carry):
            relay(c, k)
            return carry

        lax.fori_loop(first, last, body, 0)

    def rows_of(parity, block):
        return pl.ds(pl.multiple_of(parity * maxlen + block * local_len, local_len), local_len)

    def region(parity, block):
        return nbuf.at[:, rows_of(parity, block), :]

    def across():
        return remote(
            nbuf.at[:, pl.ds(2 * maxlen, local_len), :], region(x, mp),
            xsend.at[0], xrecv.at[x, mp], partner, mp,
        )

    def to_mate(parity, block):
        return remote(
            region(parity, block), region(parity, block),
            xmate.at[parity, block // 2], xrecv.at[parity, block], me, mate,
        )

    def to_far(parity, step):
        return remote(
            region(parity, mp), region(parity, mp),
            xfar.at[parity, step - 1], xrecv.at[parity, mp], me, lax.rem(mp + 2 * step, n_mp),
        )

    def arrived(parity, block):
        return remote(
            region(parity, block), region(parity, block),
            xsend.at[0], xrecv.at[parity, block], me, mate,
        )

    def spread(parity):
        for step in range(1, pairs):
            to_far(parity, step).start()
        to_mate(parity, mp).start()

    def pass_on(parity):
        for step in range(1, pairs):
            block = lax.rem(mp + 2 * step, n_mp)
            arrived(parity, block).wait_recv()
            to_mate(parity, block).start()

    load_w[0].wait()
    send_own(0)
    for load in load_x:
        load.wait()
    for t in range(width // LANES):
        ngain[:, t * LANES : (t + 1) * LANES] = ngain_t[t : t + 1, :]
    total = jnp.zeros((local_len, LANES), f32)
    for t in range(width // LANES):
        rows = hid[:, t * LANES : (t + 1) * LANES].astype(f32)
        total = total + rows * rows
    scale = lax.rsqrt(jnp.sum(total, axis=-1, keepdims=True) / width + 1e-06)
    for block in range(n_dp):
        span = slice(block * fcols, (block + 1) * fcols)
        rows = hid[:, span].astype(f32)
        first = jnp.where(x == block % 2, x * maxlen + mp * local_len, 2 * maxlen)
        nbuf[block // 2, pl.ds(pl.multiple_of(first, local_len), local_len), :] = (
            rows * scale * ngain[:, span]
        ).astype(bf16)
    across().start()
    spread(x)
    for c in range(1, min(3, nc)):
        load_w[c].wait()
        send_own(c)
    acc[...] = jnp.zeros_like(acc)

    def rollout_rows(parity):
        return pl.ds(pl.multiple_of(parity * maxlen, maxlen), maxlen)

    def swap(c):
        return remote(pout.at[c], pin.at[c], qsend.at[c], qrecv.at[c], partner, mp)

    def compute(c):
        def half(parity):
            rows = rollout_rows(parity)

            def body(k, carry):
                acc[c, rows, :] += jnp.dot(
                    nbuf[k, rows, :], wbuf[k, c], preferred_element_type=f32
                )
                return carry

            lax.fori_loop(0, nz, body, 0)

        half(1 - x)
        pout[c] = acc[c, rollout_rows(1 - x), :].astype(bf16)
        swap(c).start()
        half(x)

    length = len_ref[0]
    live = lax.broadcasted_iota(jnp.int32, (maxlen, HD), 0) < length

    def rotated(block, span):
        return block * cos_ref[span, :] + pltpu.roll(block, HD // 2, 1) * sin_ref[span, :]

    everything = slice(0, maxlen)

    def keys_done():
        swap(0).wait_recv()
        for h in range(kv_heads):
            cols = slice(h * HD, (h + 1) * HD)
            raw = acc[0, rollout_rows(x), cols] + pin[0, :, cols].astype(f32)
            kbuf[:, cols] = jnp.where(live, rotated(raw, everything), 0.0).astype(bf16)

    def values_done():
        swap(1).wait_recv()
        for h in range(kv_heads):
            cols = slice(h * HD, (h + 1) * HD)
            raw = acc[1, rollout_rows(x), cols] + pin[1, :, cols].astype(f32)
            value = jnp.where(live, raw, 0.0).astype(bf16)
            vbuf[:, cols] = value
            vext[h, :, :HD] = value
            vext[h, :, HD:] = jnp.where(live, 1.0, 0.0).astype(bf16)

    def share(j, parity):
        ref = att.at[parity, :, pl.ds(j * kw, kw)]
        return remote(ref, ref, asend.at[j], arecv.at[j], partner, mp)

    def attend(j):
        swap(2 + j).wait_recv()
        for i in range(kv_heads):
            h = j * kv_heads + i
            kv = h * kv_heads // q_heads
            cols, kcols = slice(i * HD, (i + 1) * HD), slice(kv * HD, (kv + 1) * HD)
            for r in range(n_mp):
                span, seen = slice(r * local_len, (r + 1) * local_len), (r + 1) * local_len
                raw = acc[2 + j, rows_of(x, r), cols] + pin[2 + j, span, cols].astype(f32)
                query = (rotated(raw, span) * 144.0 ** (-0.5)).astype(bf16)
                score = lax.dot_general(
                    query, kbuf[:seen, kcols], (((1,), (1,)), ((), ())),
                    preferred_element_type=f32,
                )
                row = lax.broadcasted_iota(jnp.int32, score.shape, 0) + r * local_len
                col = lax.broadcasted_iota(jnp.int32, score.shape, 1)
                expo = jnp.exp2(jnp.tanh(score * (1.0 / 50.0)) * (50.0 * np.log2(np.e)))
                expo = jnp.where(col <= row, expo, 0.0).astype(bf16)
                both = jnp.dot(expo, vext[kv, :seen, :], preferred_element_type=f32)
                att[x, span, h * HD : (h + 1) * HD] = (both[:, :HD] / both[:, HD:]).astype(bf16)
        share(j, x).start()

    relays(0, 1, 2)
    arrived(1 - x, mp).wait_recv()
    spread(1 - x)
    pass_on(x)
    relays(0, 2, nz)
    pass_on(1 - x)
    for c in range(3, nc):
        load_w[c].wait()
        send_own(c)
    load_o.wait()

    @pl.when(jnp.logical_not(middle))
    def _():
        for s in range(ns):
            send_own(nc + s)

    for parity in (x, 1 - x):
        for step in range(pairs):
            arrived(parity, lax.rem(mate + 2 * step, n_mp)).wait_recv()
    compute(0)
    relays(1, 1, nz)
    compute(1)
    for load in load_r:
        load.wait()
    for t in range(width // LANES):
        pgain[:, t * LANES : (t + 1) * LANES] = pgain_t[t : t + 1, :]
    keys_done()
    for j in range(nq):
        c = 2 + j
        relays(c, 1, 2)
        if j == 0:
            relays(c, 2, nz)
            compute(c)
            values_done()
        else:
            attend(j - 1)
            relays(c, 2, nz)
            if j == nq - 1:
                @pl.when(middle)
                def _():
                    for s in range(ns):
                        send_own(nc + s)
            compute(c)
    if nq == 1:
        @pl.when(middle)
        def _():
            for s in range(ns):
                send_own(nc + s)

    out_k = pltpu.make_async_copy(kbuf, key_out, osem.at[0])
    out_v = pltpu.make_async_copy(vbuf, val_out, osem.at[1])
    out_k.start()
    out_v.start()

    def hand(s, zk, role, parity):
        return remote(
            psend[s].at[zk, parity, 1 - side], inbox[s].at[zk, parity],
            hsend.at[s, zk, role], hrecv.at[s, zk, role], me, mate,
        )

    def far(s, zk, role, parity, step):
        target = lax.rem(mp + 2 * step, n_mp)
        return remote(
            psend[s].at[zk, parity, side, target // 2], precv[s].at[zk, parity, step - 1],
            fsend.at[s, zk, role, step - 1], frecv.at[s, zk, role, step - 1], me, target,
        )

    def back(s, zk, parity):
        return remote(
            xout[s].at[zk], yall[s].at[parity, zk], csend.at[s, zk], crecv.at[s, zk], partner, mp
        )

    def parity_of(role):
        return x if role == OWN else 1 - x

    def produce(s, zk, role):
        start, size = pieces[s]
        parity = parity_of(role)
        part = lax.dot_general(
            att[parity], obuf[zk, start : start + size, :], (((1,), (1,)), ((), ())),
            preferred_element_type=f32,
        ).astype(bf16)
        for p in range(n_mp):
            psend[s][zk, parity, p % 2, p // 2] = part[p * local_len : (p + 1) * local_len]
        hand(s, zk, role, parity).start()

    def combine(s, zk, role):
        parity = parity_of(role)
        hand(s, zk, role, parity).wait_recv()
        for step in range(1, pairs):
            q = lax.rem(mp + 2 * step, n_mp) // 2
            both = psend[s][zk, parity, side, q].astype(f32) + inbox[s][zk, parity, q].astype(f32)
            psend[s][zk, parity, side, q] = both.astype(bf16)
            far(s, zk, role, parity, step).start()

    def measure(value):
        value = value.astype(f32)
        sq[...] += jnp.sum(value * value, axis=-1, keepdims=True)

    def settle(s, zk, role):
        parity = parity_of(role)
        value = psend[s][zk, parity, side, slot].astype(f32)
        value = value + inbox[s][zk, parity, slot].astype(f32)
        for step in range(1, pairs):
            far(s, zk, role, parity, step).wait_recv()
            value = value + precv[s][zk, parity, step - 1].astype(f32)
        value = value.astype(bf16)
        if role == OWN:
            yall[s][x, zk] = value
            measure(value)
        else:
            xout[s][zk] = value
            back(s, zk, x).start()

    def around(k, act):
        def body(way, carry):
            zk = z + k * (2 * way - 1)

            @pl.when((zk >= 0) & (zk < nz) & ((way == 0) | (k > 0)))
            def _():
                act(zk)

            return carry

        lax.fori_loop(0, 2, body, 0)

    def near(act):
        def body(k, carry):
            around(k, act)
            return carry

        lax.fori_loop(0, min(2, nz), body, 0)

    for s in range(ns):
        relays(nc + s, 1, min(2, nz))
    attend(nq - 1)
    sq[...] = jnp.zeros_like(sq)
    for role in (OWN, OTHER):
        if role == OTHER:
            for j in range(nq):
                share(j, 1 - x).wait_recv()
        for s in range(ns):
            near(functools.partial(produce, s, role=role))
        for s in range(ns):
            near(functools.partial(combine, s, role=role))

    def settle_near():
        for role in (OWN, OTHER):
            for s in range(ns):
                near(functools.partial(settle, s, role=role))

    def settle_at(k):
        for s in range(ns):
            def both(zk, s=s):
                for role in (OWN, OTHER):
                    settle(s, zk, role)

            around(k, both)

    def late(k, carry):
        for s in range(ns):
            if s == ns - 1:
                @pl.when(k == 2)
                def _():
                    settle_near()

                @pl.when(k > 2)
                def _():
                    settle_at(k - 1)

            relay(nc + s, k)

            def make(zk, s=s):
                for role in (OWN, OTHER):
                    produce(s, zk, role)

            def join(zk, s=s):
                for role in (OWN, OTHER):
                    combine(s, zk, role)

            around(k, make)
            around(k, join)
        return carry

    if nz > 2:
        lax.fori_loop(2, nz, late, 0)
        settle_at(nz - 1)
    else:
        settle_near()

    def collect(zk, carry):
        for s in range(ns):
            back(s, zk, 1 - x).wait_recv()
            measure(yall[s][1 - x, zk])
        return carry

    lax.fori_loop(0, nz, collect, 0)

    scale = lax.rsqrt(sq[...] / width + 1e-06)
    halves = 2
    tall = local_len // halves
    outs = []
    for part in range(halves):
        rows = slice(part * tall, (part + 1) * tall)
        for block in range(n_dp):
            for s, (start, size) in enumerate(pieces):
                span = slice(block * fcols + start, block * fcols + start + size)
                own = (
                    lax.broadcasted_iota(jnp.int32, (tall, size), 0) + mp * local_len + part * tall
                    < length
                )
                post = yall[s][block % 2, block // 2, rows, :].astype(f32)
                post = post * scale[rows] * pgain[:, span]
                mbuf[rows, span] = jnp.where(
                    own, hid[rows, span].astype(f32) + post, 0.0
                ).astype(bf16)
        out = pltpu.make_async_copy(
            mbuf.at[pl.ds(part * tall, tall)], mixed.at[pl.ds(part * tall, tall)],
            osem.at[2 + part],
        )
        out.start()
        outs.append(out)

    def drain_items(origin, carry):
        for c in range(nc + ns):
            @pl.when((origin <= z) & can_up)
            def _():
                copy(c, origin, UP).wait_send()

            @pl.when((origin >= z) & can_down)
            def _():
                copy(c, origin, DOWN).wait_send()

        for s in range(ns):
            for role in (OWN, OTHER):
                parity = parity_of(role)
                hand(s, origin, role, parity).wait_send()
                for step in range(1, pairs):
                    far(s, origin, role, parity, step).wait_send()
            back(s, origin, x).wait_send()
        return carry

    lax.fori_loop(0, nz, drain_items, 0)
    across().wait_send()
    for parity in (x, 1 - x):
        for step in range(1, pairs):
            to_far(parity, step).wait_send()
        for step in range(pairs):
            to_mate(parity, lax.rem(mp + 2 * step, n_mp)).wait_send()
    for c in range(nc):
        swap(c).wait_send()
    for j in range(nq):
        share(j, x).wait_send()
    for out in [out_k, out_v] + outs:
        out.wait()


def local(n_dp, n_mp, hidden, lengths, norm_gain, w_query, w_key, w_value, w_out, post_gain):
    _, local_len, width = hidden.shape
    maxlen = local_len * n_mp
    rows, qw = w_query.shape
    kw = w_key.shape[1]
    orows, fcols = w_out.shape
    nz, pairs = n_dp // 2, n_mp // 2
    far = max(1, pairs - 1)
    nq = qw // kw
    nc = 2 + nq
    pieces = cut(fcols)
    ns = len(pieces)
    cosine, sine = tables(maxlen)
    anywhere = pl.BlockSpec(memory_space=pl.ANY)
    bf16, f32 = jnp.bfloat16, jnp.float32
    dma = pltpu.SemaphoreType.DMA
    tiles = (width // LANES, LANES)

    def per_piece(*lead):
        return [pltpu.VMEM((*lead, local_len, size), bf16) for _, size in pieces]

    mixed, keys, values = pl.pallas_call(
        functools.partial(kernel, n_dp, n_mp, pieces),
        out_shape=(
            jax.ShapeDtypeStruct((local_len, width), bf16),
            jax.ShapeDtypeStruct((maxlen, kw), bf16),
            jax.ShapeDtypeStruct((maxlen, kw), bf16),
        ),
        in_specs=[pl.BlockSpec(memory_space=pltpu.SMEM)] + [anywhere] * 9,
        out_specs=(anywhere,) * 3,
        scratch_shapes=[
            pltpu.VMEM((local_len, width), bf16),
            pltpu.VMEM(tiles, f32),
            pltpu.VMEM(tiles, f32),
            pltpu.VMEM((1, width), f32),
            pltpu.VMEM((1, width), f32),
            pltpu.VMEM((maxlen, HD), f32),
            pltpu.VMEM((maxlen, HD), f32),
            pltpu.VMEM((nz, nc, rows, kw), bf16),
            pltpu.VMEM((nz, fcols, orows), bf16),
            pltpu.VMEM((nz, 2 * maxlen + local_len, rows), bf16),
            pltpu.VMEM((nc, 2 * maxlen, kw), f32),
            pltpu.VMEM((nc, maxlen, kw), bf16),
            pltpu.VMEM((nc, maxlen, kw), bf16),
            pltpu.VMEM((maxlen, kw), bf16),
            pltpu.VMEM((maxlen, kw), bf16),
            pltpu.VMEM((kw // HD, maxlen, 2 * HD), bf16),
            pltpu.VMEM((2, maxlen, qw), bf16),
            pltpu.VMEM((local_len, 1), f32),
            pltpu.VMEM((local_len, width), bf16),
            *per_piece(nz, 2, 2, pairs),
            *per_piece(nz, 2, pairs),
            *per_piece(nz, 2, far),
            *per_piece(nz),
            *per_piece(2, nz),
            dma((nc + 6,)),
            dma((nc + ns, 2, nz)),
            dma((nc + ns, nz)),
            dma((1,)),
            dma((2, pairs)),
            dma((2, far)),
            dma((2, n_mp)),
            dma((nc,)),
            dma((nc,)),
            dma((nq,)),
            dma((nq,)),
            dma((ns, nz, 2)),
            dma((ns, nz, 2)),
            dma((ns, nz, 2, far)),
            dma((ns, nz, 2, far)),
            dma((ns, nz)),
            dma((ns, nz)),
            dma((4,)),
        ],
        compiler_params=pltpu.CompilerParams(
            collective_id=0, has_side_effects=True, vmem_limit_bytes=60 * 1024 * 1024
        ),
    )(
        lengths,
        hidden[0],
        norm_gain.reshape(tiles),
        w_query,
        w_key,
        w_value,
        w_out.T,
        post_gain.reshape(tiles),
        jnp.asarray(cosine),
        jnp.asarray(sine),
    )
    return mixed[None], keys[None], values[None]


def solution(mesh):
    return jax.shard_map(
        functools.partial(local, mesh.shape["dp"], mesh.shape["mp"]),
        mesh=mesh,
        in_specs=(
            P("dp", "mp", None),
            P("dp"),
            P(),
            P("dp", "mp"),
            P("dp", "mp"),
            P("dp", "mp"),
            P("mp", "dp"),
            P(),
        ),
        out_specs=(P("dp", "mp", None), P("dp", None, "mp"), P("dp", None, "mp")),
        check_vma=False,
    )
```

time: 173 us -> 143 us (0.83)
  Pallas kernels: 163 us -> 137 us
  local copies, waits for them, and re-layouts: 8.66 us -> 3.83 us
    pallas_call x1, Pallas kernels: 163 us -> 137 us  [local(): pl.pallas_call(functools.partial(kernel, n_dp, n_mp, pieces), out_shape=(...]
    reshape x2 -> x0, local copies, waits for them, and re-layouts: 2.69 us -> none  [the longest x1 1.35 us: local(): norm_gain.reshape(1, width)]
    unnamed x8 -> x7, local copies, waits for them, and re-layouts: 5.97 us -> 3.83 us
where the time goes in v1:
time: 143 us; the launch traced here: 142 us
  Pallas kernels  137 us (96%)
  local copies, waits for them, and re-layouts  3.83 us (3%)
    pallas_call x1, Pallas kernels, local(): pl.pallas_call(functools.partial(kernel, n_dp, n_mp, pieces), out_shape=(...  137 us
    unnamed x7, local copies, waits for them, and re-layouts  3.83 us

profile of v1, /device:TPU:0, one launch (start us, length us, event | category | flops | bytes accessed | tf_op | source)
XLA Modules:
  0.0 142.5 jit_solution(3571823473099779007)
XLA Ops:
  1.3 137.3 %shard_map.121 = (bf16[128,4608]{1,0:T(8,128)(2,1)}, bf16[512,256]{1,0:T(8,128)(2,1)}, bf16[512,256]{1,0:T(8,128)(2,1)}) custom-call(s32[1]{0:T(128)S(6)} %copy.16.len_ref, bf16[128,4608]{1,0:T(8,128)(2,1)} %bitcast.7, f32[36,128]{1,0:T(8,128)} %bitcast.12, bf16[576,512]{1,0:T(8,128)(2,1)} %wq.1, bf16[576,256]{1,0:T(8,128)(2,1)} %wk.1, bf16[576,256]{1,0:T(8,128)(2,1)} %wv.1, ...), custom_call_target="tpu_custom_call" | custom-call | tf_op jit(solution)/shard_map/pallas_call | solution.py:587
  138.6 0.0 copy-start.1
  138.6 0.0 copy-start
  138.6 2.4 %copy.17 = bf16[1,128,4608]{2,1,0:T(8,128)(2,1)} copy(bf16[1,128,4608]{2,1,0:T(8,128)(2,1)} %bitcast.8) | data formatting | bytes 2359296
  141.1 0.0 copy-done.1
  141.1 0.7 copy.18
  141.8 0.0 copy-done
  141.8 0.7 copy.19
Async XLA Ops:
  138.6 2.4 %copy-start.1 = (bf16[512,256]{1,0:T(8,128)(2,1)S(1)}, bf16[512,256]{1,0:T(8,128)(2,1)}, u32[]{:S(2)}) copy-start(bf16[512,256]{1,0:T(8,128)(2,1)} %get-tuple-element.7) | copy-start | bytes 786436
  138.6 3.1 %copy-start = (bf16[512,256]{1,0:T(8,128)(2,1)S(1)}, bf16[512,256]{1,0:T(8,128)(2,1)}, u32[]{:S(2)}) copy-start(bf16[512,256]{1,0:T(8,128)(2,1)} %get-tuple-element.8) | copy-start | bytes 786436

commit v2 on v1

--- a/solution.py
+++ b/solution.py
@@ -38,19 +38,21 @@
 def kernel(
     n_dp, n_mp, pieces,
     len_ref, hid_in, ngain_in, wq, wk, wv, wo, pgain_in, cos_in, sin_in,
-    mixed, key_out, val_out,
+    mbuf, kbuf, vbuf,
     *scratch,
 ):
     ns = len(pieces)
     (
         hid, ngain_t, pgain_t, ngain, pgain, cos_ref, sin_ref,
-        wbuf, obuf, nbuf, acc, pout, pin, kbuf, vbuf, vext, att, sq, mbuf,
-    ) = scratch[:19]
-    rest = scratch[19:]
+        wbuf, obuf, nbuf, acc, pout, pin, vext, att, sq,
+        hrows, hacc, hpout, hpin, hsum, epin,
+    ) = scratch[:22]
+    rest = scratch[22:]
     psend, inbox, precv, xout, yall = (rest[i * ns : (i + 1) * ns] for i in range(5))
     (
         load_sem, zsend, zrecv, xsend, xmate, xfar, xrecv, qsend, qrecv, asend, arecv,
-        hsend, hrecv, fsend, frecv, csend, crecv, osem,
+        hsend, hrecv, fsend, frecv, csend, crecv,
+        lsend, lmate, lfar, lrecv, bsend, brecv, esend, erecv,
     ) = rest[5 * ns :]
 
     nz = n_dp // 2
@@ -63,12 +65,22 @@
     local_len, width = hid.shape
     maxlen = local_len * n_mp
     fcols = width // n_dp
+    rows_each = wq.shape[0]
     qw, kw = wq.shape[1], wk.shape[1]
     nq = qw // kw
     nc = 2 + nq
+    at_k, at_v = 1, 2
+    at_q = [0] + list(range(3, nc))
+    lent = (at_k, at_v)
+    half = nz // 2
     q_heads, kv_heads = qw // HD, kw // HD
     can_up, can_down = z < nz - 1, z > 0
     middle = can_up & can_down
+    ends = jnp.logical_not(middle)
+    helps = (z == 1) | (z == nz - 2)
+    far_half = jnp.where((z == 0) | (z == 1), 1, 0)
+    inward = jnp.where(z == 0, me + 2, me - 2)
+    outward = jnp.where(z == 1, me - 2, me + 2)
     f32, bf16 = jnp.float32, jnp.bfloat16
 
     def remote(src, dst, send, recv, dp_index, mp_index):
@@ -77,12 +89,20 @@
             device_id=(dp_index, mp_index), device_id_type=MESH,
         )
 
+    def item(c, origin):
+        if c < nc:
+            first = pl.multiple_of(origin % half * rows_each, rows_each)
+            return wbuf.at[c, origin // half, pl.ds(first, rows_each)]
+        start, size = pieces[c - nc]
+        return obuf.at[origin, pl.ds(start, size)]
+
+    sources = [None] * nc
+    sources[at_k], sources[at_v] = wk, wv
+    for j, c in enumerate(at_q):
+        sources[c] = wq.at[:, pl.ds(j * kw, kw)]
     load_w = [
-        pltpu.make_async_copy(wk, wbuf.at[z, 0], load_sem.at[0]),
-        pltpu.make_async_copy(wv, wbuf.at[z, 1], load_sem.at[1]),
-    ] + [
-        pltpu.make_async_copy(wq.at[:, pl.ds(j * kw, kw)], wbuf.at[z, 2 + j], load_sem.at[2 + j])
-        for j in range(nq)
+        pltpu.make_async_copy(source, item(c, z), load_sem.at[c])
+        for c, source in enumerate(sources)
     ]
     load_o = pltpu.make_async_copy(wo, obuf.at[z], load_sem.at[nc])
     load_x = [
@@ -118,46 +138,50 @@
         barrier, n_mp + jnp.where(can_up, 1, 0) + jnp.where(can_down, 1, 0)
     )
 
-    def item(c, origin):
-        if c < nc:
-            return wbuf.at[origin, c]
-        start, size = pieces[c - nc]
-        return obuf.at[origin, pl.ds(start, size)]
-
     def copy(c, origin, way):
         ref = item(c, origin)
         return remote(
-            ref, ref, zsend.at[c, way, origin], zrecv.at[c, origin],
+            ref, ref, zsend.at[1 if c in lent else 0, way, origin], zrecv.at[c, origin],
             (me + 2, me - 2)[way], mp,
         )
 
+    def sends(c, origin, way):
+        if way == UP:
+            skip, able = (z + 1 == nz - 1) & (origin < half), can_up
+        else:
+            skip, able = (z - 1 == 0) & (origin >= half), can_down
+        return able & jnp.logical_not(skip) if c in lent else able
+
+    def gets(c, origin):
+        if c not in lent:
+            return (origin >= 0) & (origin < nz)
+        low, high = jnp.where(z == nz - 1, half, 0), jnp.where(z == 0, half, nz)
+        return (origin >= low) & (origin < high)
+
+    def send(c, origin, way):
+        @pl.when(sends(c, origin, way))
+        def _():
+            copy(c, origin, way).start()
+
     def send_own(c):
-        @pl.when(can_up)
+        send(c, z, UP)
+        send(c, z, DOWN)
+
+    def send_own_out(c, down, up):
+        @pl.when(down & middle)
+        def _():
+            copy(c, z, DOWN).start()
+
+        @pl.when(up & middle)
         def _():
             copy(c, z, UP).start()
 
-        @pl.when(can_down)
-        def _():
-            copy(c, z, DOWN).start()
-
     def relay(c, k):
-        below, above = z - k, z + k
-
-        @pl.when(below >= 0)
-        def _():
-            copy(c, below, UP).wait_recv()
-
-            @pl.when(can_up)
+        for origin, way in ((z - k, UP), (z + k, DOWN)):
+            @pl.when(gets(c, origin))
             def _():
-                copy(c, below, UP).start()
-
-        @pl.when(above < nz)
-        def _():
-            copy(c, above, DOWN).wait_recv()
-
-            @pl.when(can_down)
-            def _():
-                copy(c, above, DOWN).start()
+                copy(c, origin, way).wait_recv()
+                send(c, origin, way)
 
     def relays(c, first, last):
         def body(k, carry):
@@ -206,6 +230,38 @@
             block = lax.rem(mp + 2 * step, n_mp)
             arrived(parity, block).wait_recv()
             to_mate(parity, block).start()
+
+    def lend(parity):
+        return remote(
+            nbuf.at[far_half, rows_of(parity, mp), :],
+            hrows.at[rows_of(parity, mp), :],
+            lsend.at[parity], lrecv.at[parity, mp], inward, mp,
+        )
+
+    def lent_to(parity, block, dst, send_sem):
+        ref = hrows.at[rows_of(parity, block), :]
+        return remote(ref, ref, send_sem, lrecv.at[parity, block], me, dst)
+
+    def lent_mate(parity, block):
+        return lent_to(parity, block, mate, lmate.at[parity, block // 2])
+
+    def lent_far(parity, step):
+        return lent_to(parity, mp, lax.rem(mp + 2 * step, n_mp), lfar.at[parity, step - 1])
+
+    def lent_wait(parity, block):
+        lent_to(parity, block, mate, lsend.at[parity]).wait_recv()
+
+    def lent_spread(parity):
+        lent_wait(parity, mp)
+        for step in range(1, pairs):
+            lent_far(parity, step).start()
+        lent_mate(parity, mp).start()
+
+    def lent_pass(parity):
+        for step in range(1, pairs):
+            block = lax.rem(mp + 2 * step, n_mp)
+            lent_wait(parity, block)
+            lent_mate(parity, block).start()
 
     load_w[0].wait()
     send_own(0)
@@ -222,15 +278,25 @@
         span = slice(block * fcols, (block + 1) * fcols)
         rows = hid[:, span].astype(f32)
         first = jnp.where(x == block % 2, x * maxlen + mp * local_len, 2 * maxlen)
-        nbuf[block // 2, pl.ds(pl.multiple_of(first, local_len), local_len), :] = (
+        k = block // 2
+        cols = slice(k % half * fcols, (k % half + 1) * fcols)
+        nbuf[k // half, pl.ds(pl.multiple_of(first, local_len), local_len), cols] = (
             rows * scale * ngain[:, span]
         ).astype(bf16)
     across().start()
     spread(x)
-    for c in range(1, min(3, nc)):
-        load_w[c].wait()
-        send_own(c)
+
+    @pl.when(ends)
+    def _():
+        lend(x).start()
+
+    load_w[1].wait()
+    send_own(1)
     acc[...] = jnp.zeros_like(acc)
+
+    @pl.when(middle)
+    def _():
+        epin[...] = jnp.zeros_like(epin)
 
     def rollout_rows(parity):
         return pl.ds(pl.multiple_of(parity * maxlen, maxlen), maxlen)
@@ -239,21 +305,57 @@
         return remote(pout.at[c], pin.at[c], qsend.at[c], qrecv.at[c], partner, mp)
 
     def compute(c):
-        def half(parity):
+        first, last = 0, 2
+        if c in lent:
+            first, last = jnp.where(z == nz - 1, 1, 0), jnp.where(z == 0, 1, 2)
+
+        def contract(parity):
             rows = rollout_rows(parity)
 
             def body(k, carry):
                 acc[c, rows, :] += jnp.dot(
-                    nbuf[k, rows, :], wbuf[k, c], preferred_element_type=f32
+                    nbuf[k, rows, :], wbuf[c, k], preferred_element_type=f32
                 )
                 return carry
 
-            lax.fori_loop(0, nz, body, 0)
-
-        half(1 - x)
+            lax.fori_loop(first, last, body, 0)
+
+        contract(1 - x)
         pout[c] = acc[c, rollout_rows(1 - x), :].astype(bf16)
         swap(c).start()
-        half(x)
+        contract(x)
+
+    def lent_swap(i):
+        return remote(hpout.at[i], hpin.at[i], bsend.at[i], brecv.at[i], partner, mp)
+
+    def lent_return(i):
+        return remote(hsum.at[i], epin.at[i], esend.at[i], erecv.at[i], outward, mp)
+
+    def lent_compute(i):
+        def contract(parity):
+            rows = rollout_rows(parity)
+
+            hacc[i, rows, :] = jnp.dot(
+                hrows[rows, :], wbuf[lent[i], far_half], preferred_element_type=f32
+            )
+
+        contract(1 - x)
+        hpout[i] = hacc[i, rollout_rows(1 - x), :].astype(bf16)
+        lent_swap(i).start()
+        contract(x)
+
+    def lent_finish(i):
+        lent_swap(i).wait_recv()
+        hsum[i] = (hacc[i, rollout_rows(x), :] + hpin[i].astype(f32)).astype(bf16)
+        lent_return(i).start()
+
+    def lent_add(i, cols):
+        return epin[i, :, cols].astype(f32)
+
+    def lent_ready(i):
+        @pl.when(ends)
+        def _():
+            lent_return(i).wait_recv()
 
     length = len_ref[0]
     live = lax.broadcasted_iota(jnp.int32, (maxlen, HD), 0) < length
@@ -264,17 +366,21 @@
     everything = slice(0, maxlen)
 
     def keys_done():
-        swap(0).wait_recv()
+        swap(at_k).wait_recv()
+        lent_ready(0)
         for h in range(kv_heads):
             cols = slice(h * HD, (h + 1) * HD)
-            raw = acc[0, rollout_rows(x), cols] + pin[0, :, cols].astype(f32)
+            raw = acc[at_k, rollout_rows(x), cols] + pin[at_k, :, cols].astype(f32)
+            raw = raw + lent_add(0, cols)
             kbuf[:, cols] = jnp.where(live, rotated(raw, everything), 0.0).astype(bf16)
 
     def values_done():
-        swap(1).wait_recv()
+        swap(at_v).wait_recv()
+        lent_ready(1)
         for h in range(kv_heads):
             cols = slice(h * HD, (h + 1) * HD)
-            raw = acc[1, rollout_rows(x), cols] + pin[1, :, cols].astype(f32)
+            raw = acc[at_v, rollout_rows(x), cols] + pin[at_v, :, cols].astype(f32)
+            raw = raw + lent_add(1, cols)
             value = jnp.where(live, raw, 0.0).astype(bf16)
             vbuf[:, cols] = value
             vext[h, :, :HD] = value
@@ -285,14 +391,14 @@
         return remote(ref, ref, asend.at[j], arecv.at[j], partner, mp)
 
     def attend(j):
-        swap(2 + j).wait_recv()
+        swap(at_q[j]).wait_recv()
         for i in range(kv_heads):
             h = j * kv_heads + i
             kv = h * kv_heads // q_heads
             cols, kcols = slice(i * HD, (i + 1) * HD), slice(kv * HD, (kv + 1) * HD)
             for r in range(n_mp):
                 span, seen = slice(r * local_len, (r + 1) * local_len), (r + 1) * local_len
-                raw = acc[2 + j, rows_of(x, r), cols] + pin[2 + j, span, cols].astype(f32)
+                raw = acc[at_q[j], rows_of(x, r), cols] + pin[at_q[j], span, cols].astype(f32)
                 query = (rotated(raw, span) * 144.0 ** (-0.5)).astype(bf16)
                 score = lax.dot_general(
                     query, kbuf[:seen, kcols], (((1,), (1,)), ((), ())),
@@ -309,73 +415,114 @@
     relays(0, 1, 2)
     arrived(1 - x, mp).wait_recv()
     spread(1 - x)
+
+    @pl.when(ends)
+    def _():
+        lend(1 - x).start()
+
+    for load in load_w[2:] + [load_o]:
+        load.wait()
+    send_own(2)
+
+    @pl.when(ends)
+    def _():
+        for c in range(3, nc + ns):
+            send_own(c)
+
     pass_on(x)
+
+    @pl.when(helps)
+    def _():
+        lent_spread(x)
+
     relays(0, 2, nz)
+    relays(1, 1, 2)
+    @pl.when(middle)
+    def _():
+        for c in range(3, nc):
+            send_own(c)
+
+    early = {0, ns - 1}
+    for s in sorted(early):
+        send_own_out(nc + s, z == 1, z == nz - 2)
+
+    @pl.when(helps)
+    def _():
+        lent_spread(1 - x)
+
     pass_on(1 - x)
-    for c in range(3, nc):
-        load_w[c].wait()
-        send_own(c)
-    load_o.wait()
-
-    @pl.when(jnp.logical_not(middle))
-    def _():
-        for s in range(ns):
-            send_own(nc + s)
-
     for parity in (x, 1 - x):
         for step in range(pairs):
             arrived(parity, lax.rem(mate + 2 * step, n_mp)).wait_recv()
     compute(0)
-    relays(1, 1, nz)
+
+    @pl.when(helps)
+    def _():
+        lent_pass(x)
+
+    relays(1, 2, nz)
+    relays(2, 1, 2)
     compute(1)
+
+    @pl.when(helps)
+    def _():
+        lent_pass(1 - x)
+        for parity in (x, 1 - x):
+            for step in range(pairs):
+                lent_wait(parity, lax.rem(mate + 2 * step, n_mp))
+        lent_compute(0)
+
+    for c in range(3, nc):
+        relays(c, 1, 2)
     for load in load_r:
         load.wait()
     for t in range(width // LANES):
         pgain[:, t * LANES : (t + 1) * LANES] = pgain_t[t : t + 1, :]
+    relays(2, 2, nz)
+
+    @pl.when(helps)
+    def _():
+        lent_compute(1)
+
+    compute(2)
+
+    @pl.when(helps)
+    def _():
+        lent_finish(0)
+
+    for c in range(3, nc):
+        relays(c, 2, nz)
+        compute(c)
+
+    @pl.when(helps)
+    def _():
+        lent_finish(1)
+
+    for s in range(ns):
+        sent_out = s in early
+        send_own_out(nc + s, z != 1 if sent_out else True, z != nz - 2 if sent_out else True)
+
     keys_done()
-    for j in range(nq):
-        c = 2 + j
-        relays(c, 1, 2)
-        if j == 0:
-            relays(c, 2, nz)
-            compute(c)
-            values_done()
-        else:
-            attend(j - 1)
-            relays(c, 2, nz)
-            if j == nq - 1:
-                @pl.when(middle)
-                def _():
-                    for s in range(ns):
-                        send_own(nc + s)
-            compute(c)
-    if nq == 1:
-        @pl.when(middle)
-        def _():
-            for s in range(ns):
-                send_own(nc + s)
-
-    out_k = pltpu.make_async_copy(kbuf, key_out, osem.at[0])
-    out_v = pltpu.make_async_copy(vbuf, val_out, osem.at[1])
-    out_k.start()
-    out_v.start()
+    values_done()
+    for j in range(nq - 1):
+        attend(j)
 
     def hand(s, zk, role, parity):
         return remote(
             psend[s].at[zk, parity, 1 - side], inbox[s].at[zk, parity],
-            hsend.at[s, zk, role], hrecv.at[s, zk, role], me, mate,
+            hsend.at[s], hrecv.at[s, zk, role], me, mate,
         )
 
     def far(s, zk, role, parity, step):
         target = lax.rem(mp + 2 * step, n_mp)
         return remote(
             psend[s].at[zk, parity, side, target // 2], precv[s].at[zk, parity, step - 1],
-            fsend.at[s, zk, role, step - 1], frecv.at[s, zk, role, step - 1], me, target,
+            fsend.at[s], frecv.at[s, zk, role, step - 1], me, target,
         )
 
     def back(s, zk, parity):
         return remote(
-            xout[s].at[zk], yall[s].at[parity, zk], csend.at[s, zk], crecv.at[s, zk], partner, mp
+            xout[s].at[zk], yall[s].at[parity, zk], csend.at[s], crecv.at[s], partner, mp
         )
 
     def parity_of(role):
@@ -439,116 +586,108 @@
 
         lax.fori_loop(0, min(2, nz), body, 0)
 
-    for s in range(ns):
-        relays(nc + s, 1, min(2, nz))
     attend(nq - 1)
     sq[...] = jnp.zeros_like(sq)
-    for role in (OWN, OTHER):
-        if role == OTHER:
-            for j in range(nq):
-                share(j, 1 - x).wait_recv()
-        for s in range(ns):
-            near(functools.partial(produce, s, role=role))
-        for s in range(ns):
-            near(functools.partial(combine, s, role=role))
+    for s in range(ns):
+        produce(s, z, OWN)
+    for s in range(ns):
+        relays(nc + s, 1, 2)
+        combine(s, z, OWN)
+    for s in range(ns):
+        around(1, functools.partial(produce, s, role=OWN))
+    for s in range(ns):
+        around(1, functools.partial(combine, s, role=OWN))
+    for j in range(nq):
+        share(j, 1 - x).wait_recv()
+    for s in range(ns):
+        near(functools.partial(produce, s, role=OTHER))
+    for s in range(ns):
+        near(functools.partial(combine, s, role=OTHER))
 
     def settle_near():
-        for role in (OWN, OTHER):
+        for role in (OTHER, OWN):
             for s in range(ns):
                 near(functools.partial(settle, s, role=role))
 
-    def settle_at(k):
-        for s in range(ns):
-            def both(zk, s=s):
-                for role in (OWN, OTHER):
-                    settle(s, zk, role)
-
-            around(k, both)
+    def settle_at(s, k):
+        def both(zk):
+            for role in (OTHER, OWN):
+                settle(s, zk, role)
+
+        around(k, both)
 
     def late(k, carry):
         for s in range(ns):
-            if s == ns - 1:
+            relay(nc + s, k)
+
+            def make(zk, s=s):
+                for role in (OTHER, OWN):
+                    produce(s, zk, role)
+
+            def join(zk, s=s):
+                for role in (OTHER, OWN):
+                    combine(s, zk, role)
+
+            around(k, make)
+            around(k, join)
+            if s > 0:
+                settle_at(s - 1, k)
+            else:
                 @pl.when(k == 2)
                 def _():
                     settle_near()
 
                 @pl.when(k > 2)
                 def _():
-                    settle_at(k - 1)
-
-            relay(nc + s, k)
-
-            def make(zk, s=s):
-                for role in (OWN, OTHER):
-                    produce(s, zk, role)
-
-            def join(zk, s=s):
-                for role in (OWN, OTHER):
-                    combine(s, zk, role)
-
-            around(k, make)
-            around(k, join)
+                    settle_at(ns - 1, k - 1)
+
         return carry
 
     if nz > 2:
         lax.fori_loop(2, nz, late, 0)
-        settle_at(nz - 1)
+        settle_at(ns - 1, nz - 1)
     else:
         settle_near()
 
+    for s in range(ns):
+        remote(xout[s], yall[s].at[1 - x], csend.at[s], crecv.at[s], partner, mp).wait_recv()
+
     def collect(zk, carry):
         for s in range(ns):
-            back(s, zk, 1 - x).wait_recv()
             measure(yall[s][1 - x, zk])
         return carry
 
     lax.fori_loop(0, nz, collect, 0)
 
     scale = lax.rsqrt(sq[...] / width + 1e-06)
-    halves = 2
-    tall = local_len // halves
-    outs = []
-    for part in range(halves):
-        rows = slice(part * tall, (part + 1) * tall)
-        for block in range(n_dp):
-            for s, (start, size) in enumerate(pieces):
-                span = slice(block * fcols + start, block * fcols + start + size)
-                own = (
-                    lax.broadcasted_iota(jnp.int32, (tall, size), 0) + mp * local_len + part * tall
-                    < length
-                )
-                post = yall[s][block % 2, block // 2, rows, :].astype(f32)
-                post = post * scale[rows] * pgain[:, span]
-                mbuf[rows, span] = jnp.where(
-                    own, hid[rows, span].astype(f32) + post, 0.0
-                ).astype(bf16)
-        out = pltpu.make_async_copy(
-            mbuf.at[pl.ds(part * tall, tall)], mixed.at[pl.ds(part * tall, tall)],
-            osem.at[2 + part],
-        )
-        out.start()
-        outs.append(out)
+    for block in range(n_dp):
+        for s, (start, size) in enumerate(pieces):
+            span = slice(block * fcols + start, block * fcols + start + size)
+            own = lax.broadcasted_iota(jnp.int32, (local_len, size), 0) + mp * local_len < length
+            post = yall[s][block % 2, block // 2].astype(f32) * scale * pgain[:, span]
+            mbuf[:, span] = jnp.where(own, hid[:, span].astype(f32) + post, 0.0).astype(bf16)
+
+    def sent(ref, sem):
+        remote(ref, ref, sem, sem, partner, mp).wait_send()
 
     def drain_items(origin, carry):
-        for c in range(nc + ns):
-            @pl.when((origin <= z) & can_up)
+        for way, mine in ((UP, origin <= z), (DOWN, origin >= z)):
+            @pl.when(mine & sends(nc, origin, way))
             def _():
-                copy(c, origin, UP).wait_send()
-
-            @pl.when((origin >= z) & can_down)
+                sent(obuf.at[pl.ds(0, 2)], zsend.at[0, way, origin])
+
+            @pl.when(mine & sends(at_k, origin, way))
             def _():
-                copy(c, origin, DOWN).wait_send()
-
-        for s in range(ns):
-            for role in (OWN, OTHER):
-                parity = parity_of(role)
-                hand(s, origin, role, parity).wait_send()
-                for step in range(1, pairs):
-                    far(s, origin, role, parity, step).wait_send()
-            back(s, origin, x).wait_send()
+                sent(wbuf.at[pl.ds(at_k, 2), 0, pl.ds(0, rows_each)], zsend.at[1, way, origin])
+
         return carry
 
     lax.fori_loop(0, nz, drain_items, 0)
+    for s in range(ns):
+        sent(psend[s].at[:, :, 0], hsend.at[s])
+        if pairs > 1:
+            sent(precv[s], fsend.at[s])
+        sent(xout[s], csend.at[s])
     across().wait_send()
     for parity in (x, 1 - x):
         for step in range(1, pairs):
@@ -557,10 +696,25 @@
             to_mate(parity, lax.rem(mp + 2 * step, n_mp)).wait_send()
     for c in range(nc):
         swap(c).wait_send()
+
+    @pl.when(ends)
+    def _():
+        for parity in range(2):
+            lend(parity).wait_send()
+
+    @pl.when(helps)
+    def _():
+        for parity in (x, 1 - x):
+            for step in range(1, pairs):
+                lent_far(parity, step).wait_send()
+            for step in range(pairs):
+                lent_mate(parity, lax.rem(mp + 2 * step, n_mp)).wait_send()
+        for i in range(len(lent)):
+            lent_swap(i).wait_send()
+            lent_return(i).wait_send()
+
     for j in range(nq):
         share(j, x).wait_send()
-    for out in [out_k, out_v] + outs:
-        out.wait()
 
 
 def local(n_dp, n_mp, hidden, lengths, norm_gain, w_query, w_key, w_value, w_out, post_gain):
@@ -587,12 +741,12 @@
     mixed, keys, values = pl.pallas_call(
         functools.partial(kernel, n_dp, n_mp, pieces),
         out_shape=(
-            jax.ShapeDtypeStruct((local_len, width), bf16),
-            jax.ShapeDtypeStruct((maxlen, kw), bf16),
-            jax.ShapeDtypeStruct((maxlen, kw), bf16),
+            pltpu.VMEM((local_len, width), bf16),
+            pltpu.VMEM((maxlen, kw), bf16),
+            pltpu.VMEM((maxlen, kw), bf16),
         ),
         in_specs=[pl.BlockSpec(memory_space=pltpu.SMEM)] + [anywhere] * 9,
-        out_specs=(anywhere,) * 3,
+        out_specs=(pl.BlockSpec(memory_space=pltpu.VMEM),) * 3,
         scratch_shapes=[
             pltpu.VMEM((local_len, width), bf16),
             pltpu.VMEM(tiles, f32),
@@ -601,25 +755,28 @@
             pltpu.VMEM((1, width), f32),
             pltpu.VMEM((maxlen, HD), f32),
             pltpu.VMEM((maxlen, HD), f32),
-            pltpu.VMEM((nz, nc, rows, kw), bf16),
+            pltpu.VMEM((nc, 2, nz // 2 * rows, kw), bf16),
             pltpu.VMEM((nz, fcols, orows), bf16),
-            pltpu.VMEM((nz, 2 * maxlen + local_len, rows), bf16),
+            pltpu.VMEM((2, 2 * maxlen + local_len, nz // 2 * rows), bf16),
             pltpu.VMEM((nc, 2 * maxlen, kw), f32),
             pltpu.VMEM((nc, maxlen, kw), bf16),
             pltpu.VMEM((nc, maxlen, kw), bf16),
-            pltpu.VMEM((maxlen, kw), bf16),
-            pltpu.VMEM((maxlen, kw), bf16),
             pltpu.VMEM((kw // HD, maxlen, 2 * HD), bf16),
             pltpu.VMEM((2, maxlen, qw), bf16),
             pltpu.VMEM((local_len, 1), f32),
-            pltpu.VMEM((local_len, width), bf16),
+            pltpu.VMEM((2 * maxlen, nz // 2 * rows), bf16),
+            pltpu.VMEM((2, 2 * maxlen, kw), f32),
+            pltpu.VMEM((2, maxlen, kw), bf16),
+            pltpu.VMEM((2, maxlen, kw), bf16),
+            pltpu.VMEM((2, maxlen, kw), bf16),
+            pltpu.VMEM((2, maxlen, kw), bf16),
             *per_piece(nz, 2, 2, pairs),
             *per_piece(nz, 2, pairs),
             *per_piece(nz, 2, far),
             *per_piece(nz),
             *per_piece(2, nz),
             dma((nc + 6,)),
-            dma((nc + ns, 2, nz)),
+            dma((2, 2, nz)),
             dma((nc + ns, nz)),
             dma((1,)),
             dma((2, pairs)),
@@ -629,13 +786,20 @@
             dma((nc,)),
             dma((nq,)),
             dma((nq,)),
+            dma((ns,)),
             dma((ns, nz, 2)),
-            dma((ns, nz, 2)),
+            dma((ns,)),
             dma((ns, nz, 2, far)),
-            dma((ns, nz, 2, far)),
-            dma((ns, nz)),
-            dma((ns, nz)),
-            dma((4,)),
+            dma((ns,)),
+            dma((ns,)),
+            dma((2,)),
+            dma((2, pairs)),
+            dma((2, far)),
+            dma((2, n_mp)),
+            dma((2,)),
+            dma((2,)),
+            dma((2,)),
+            dma((2,)),
         ],
         compiler_params=pltpu.CompilerParams(
             collective_id=0, has_side_effects=True, vmem_limit_bytes=60 * 1024 * 1024

time: 143 us -> 129 us (0.902)
  Pallas kernels: 137 us -> 125 us
    pallas_call x1, Pallas kernels: 137 us -> 125 us  [local(): pl.pallas_call(functools.partial(kernel, n_dp, n_mp, pieces), out_shape=(...]
    unnamed x7 -> x3, local copies, waits for them, and re-layouts: 3.83 us -> 2.42 us
where the time goes in v2:
time: 129 us
  Pallas kernels  125 us (97%)
  local copies, waits for them, and re-layouts  2.42 us (2%)
  between operations  1.29 us (1%)
    pallas_call x1, Pallas kernels, local(): pl.pallas_call(functools.partial(kernel, n_dp, n_mp, pieces), out_shape=(...  125 us

profile of v2, /device:TPU:0, one launch (start us, length us, event | category | flops | bytes accessed | tf_op | source)
XLA Modules:
  0.0 129.2 jit_solution(11337156622036698896)
XLA Ops:
  1.3 125.5 %shard_map.121 = (bf16[128,4608]{1,0:T(8,128)(2,1)S(1)}, bf16[512,256]{1,0:T(8,128)(2,1)S(1)}, bf16[512,256]{1,0:T(8,128)(2,1)S(1)}) custom-call(s32[1]{0:T(128)S(6)} %copy.19.len_ref, bf16[128,4608]{1,0:T(8,128)(2,1)} %bitcast.10, f32[36,128]{1,0:T(8,128)} %bitcast.12, bf16[576,512]{1,0:T(8,128)(2,1)} %wq.1, bf16[576,256]{1,0:T(8,128)(2,1)} %wk.1, ...), custom_call_target="tpu_custom_call" | custom-call | tf_op jit(solution)/shard_map/pallas_call | solution.py:741
  126.8 1.0 copy.16
  127.8 0.7 copy.17
  128.5 0.7 copy.18

commit v3 on v2

--- a/solution.py
+++ b/solution.py
@@ -630,24 +630,23 @@
 
             around(k, make)
             around(k, join)
-            if s > 0:
-                settle_at(s - 1, k)
-            else:
-                @pl.when(k == 2)
+            if s == 0:
+                @pl.when(k == 3)
                 def _():
                     settle_near()
 
-                @pl.when(k > 2)
-                def _():
-                    settle_at(ns - 1, k - 1)
+            @pl.when(k > 2)
+            def _():
+                settle_at(s, k - 1)
 
         return carry
 
+    lax.fori_loop(2, nz, late, 0)
+    if nz < 4:
+        settle_near()
     if nz > 2:
-        lax.fori_loop(2, nz, late, 0)
-        settle_at(ns - 1, nz - 1)
-    else:
-        settle_near()
+        for s in range(ns):
+            settle_at(s, nz - 1)
 
     for s in range(ns):
         remote(xout[s], yall[s].at[1 - x], csend.at[s], crecv.at[s], partner, mp).wait_recv()

time: 129 us -> 124 us (0.961)
  Pallas kernels: 125 us -> 120 us
    pallas_call x1, Pallas kernels: 125 us -> 120 us  [local(): pl.pallas_call(functools.partial(kernel, n_dp, n_mp, pieces), out_shape=(...]
where the time goes in v3:
time: 124 us
  Pallas kernels  120 us (97%)
  local copies, waits for them, and re-layouts  2.42 us (2%)
  between operations  1.29 us (1%)
    pallas_call x1, Pallas kernels, local(): pl.pallas_call(functools.partial(kernel, n_dp, n_mp, pieces), out_shape=(...  120 us

profile of v3, /device:TPU:0, one launch (start us, length us, event | category | flops | bytes accessed | tf_op | source)
XLA Modules:
  0.0 124.1 jit_solution(7954448507334055003)
XLA Ops:
  1.3 120.4 %shard_map.121 = (bf16[128,4608]{1,0:T(8,128)(2,1)S(1)}, bf16[512,256]{1,0:T(8,128)(2,1)S(1)}, bf16[512,256]{1,0:T(8,128)(2,1)S(1)}) custom-call(s32[1]{0:T(128)S(6)} %copy.19.len_ref, bf16[128,4608]{1,0:T(8,128)(2,1)} %bitcast.10, f32[36,128]{1,0:T(8,128)} %bitcast.12, bf16[576,512]{1,0:T(8,128)(2,1)} %wq.1, bf16[576,256]{1,0:T(8,128)(2,1)} %wk.1, ...), custom_call_target="tpu_custom_call" | custom-call | tf_op jit(solution)/shard_map/pallas_call | solution.py:740
  121.7 1.0 copy.16
  122.7 0.7 copy.17
  123.4 0.7 copy.18

commit v4 on v3

--- a/solution.py
+++ b/solution.py
@@ -35,9 +35,13 @@
     return pieces
 
 
+def packed(size):
+    return 2 * size <= LANES
+
+
 def kernel(
     n_dp, n_mp, pieces,
-    len_ref, hid_in, ngain_in, wq, wk, wv, wo, pgain_in, cos_in, sin_in,
+    len_in, hid_in, ngain_in, wq, wk, wv, wo, pgain_in, cos_in, sin_in,
     mbuf, kbuf, vbuf,
     *scratch,
 ):
@@ -45,9 +49,9 @@
     (
         hid, ngain_t, pgain_t, ngain, pgain, cos_ref, sin_ref,
         wbuf, obuf, nbuf, acc, pout, pin, vext, att, sq,
-        hrows, hacc, hpout, hpin, hsum, epin,
-    ) = scratch[:22]
-    rest = scratch[22:]
+        hrows, hacc, hpout, hpin, hsum, epin, len_ref,
+    ) = scratch[:23]
+    rest = scratch[23:]
     psend, inbox, precv, xout, yall = (rest[i * ns : (i + 1) * ns] for i in range(5))
     (
         load_sem, zsend, zrecv, xsend, xmate, xfar, xrecv, qsend, qrecv, asend, arecv,
@@ -113,6 +117,7 @@
         pltpu.make_async_copy(pgain_in, pgain_t, load_sem.at[nc + 3]),
         pltpu.make_async_copy(cos_in, cos_ref, load_sem.at[nc + 4]),
         pltpu.make_async_copy(sin_in, sin_ref, load_sem.at[nc + 5]),
+        pltpu.make_async_copy(len_in, len_ref, load_sem.at[nc + 6]),
     ]
     for load in load_w[:1] + load_x + load_w[1:] + [load_o] + load_r:
         load.start()
@@ -357,9 +362,6 @@
         def _():
             lent_return(i).wait_recv()
 
-    length = len_ref[0]
-    live = lax.broadcasted_iota(jnp.int32, (maxlen, HD), 0) < length
-
     def rotated(block, span):
         return block * cos_ref[span, :] + pltpu.roll(block, HD // 2, 1) * sin_ref[span, :]
 
@@ -476,6 +478,8 @@
         relays(c, 1, 2)
     for load in load_r:
         load.wait()
+    length = len_ref[0]
+    live = lax.broadcasted_iota(jnp.int32, (maxlen, HD), 0) < length
     for t in range(width // LANES):
         pgain[:, t * LANES : (t + 1) * LANES] = pgain_t[t : t + 1, :]
     relays(2, 2, nz)
@@ -525,22 +529,38 @@
             xout[s].at[zk], yall[s].at[parity, zk], csend.at[s], crecv.at[s], partner, mp
         )
 
+    def roles_of(s):
+        return (OTHER,) if packed(pieces[s][1]) else (OTHER, OWN)
+
     def parity_of(role):
         return x if role == OWN else 1 - x
 
+    def lead_of(s, role):
+        return 0 if packed(pieces[s][1]) else parity_of(role)
+
     def produce(s, zk, role):
         start, size = pieces[s]
-        parity = parity_of(role)
-        part = lax.dot_general(
-            att[parity], obuf[zk, start : start + size, :], (((1,), (1,)), ((), ())),
-            preferred_element_type=f32,
-        ).astype(bf16)
+        lead = lead_of(s, role)
+
+        def project(parity, weights):
+            return lax.dot_general(
+                att[parity], weights, (((1,), (1,)), ((), ())), preferred_element_type=f32
+            )
+
+        weights = obuf[zk, start : start + size, :]
+        if packed(size):
+            blank = jnp.zeros_like(weights)
+            part = project(0, jnp.concatenate([weights, blank], axis=0))
+            part = part + project(1, jnp.concatenate([blank, weights], axis=0))
+        else:
+            part = project(lead, weights)
+        part = part.astype(bf16)
         for p in range(n_mp):
-            psend[s][zk, parity, p % 2, p // 2] = part[p * local_len : (p + 1) * local_len]
-        hand(s, zk, role, parity).start()
+            psend[s][zk, lead, p % 2, p // 2] = part[p * local_len : (p + 1) * local_len]
+        hand(s, zk, role, lead).start()
 
     def combine(s, zk, role):
-        parity = parity_of(role)
+        parity = lead_of(s, role)
         hand(s, zk, role, parity).wait_recv()
         for step in range(1, pairs):
             q = lax.rem(mp + 2 * step, n_mp) // 2
@@ -553,12 +573,22 @@
         sq[...] += jnp.sum(value * value, axis=-1, keepdims=True)
 
     def settle(s, zk, role):
-        parity = parity_of(role)
+        parity = lead_of(s, role)
         value = psend[s][zk, parity, side, slot].astype(f32)
         value = value + inbox[s][zk, parity, slot].astype(f32)
         for step in range(1, pairs):
             far(s, zk, role, parity, step).wait_recv()
             value = value + precv[s][zk, parity, step - 1].astype(f32)
+        size = pieces[s][1]
+        if packed(size):
+            swapped = pltpu.roll(value, size, 1)
+            ours = jnp.where(x == 0, value, swapped)[:, :size].astype(bf16)
+            theirs = jnp.where(x == 0, swapped, value)[:, :size].astype(bf16)
+            xout[s][zk] = theirs
+            back(s, zk, x).start()
+            yall[s][x, zk] = ours
+            measure(ours)
+            return
         value = value.astype(bf16)
         if role == OWN:
             yall[s][x, zk] = value
@@ -588,14 +618,16 @@
 
     attend(nq - 1)
     sq[...] = jnp.zeros_like(sq)
-    for s in range(ns):
+    single = [s for s in range(ns) if OWN in roles_of(s)]
+    for s in single:
         produce(s, z, OWN)
     for s in range(ns):
         relays(nc + s, 1, 2)
-        combine(s, z, OWN)
-    for s in range(ns):
+        if s in single:
+            combine(s, z, OWN)
+    for s in single:
         around(1, functools.partial(produce, s, role=OWN))
-    for s in range(ns):
+    for s in single:
         around(1, functools.partial(combine, s, role=OWN))
     for j in range(nq):
         share(j, 1 - x).wait_recv()
@@ -607,11 +639,16 @@
     def settle_near():
         for role in (OTHER, OWN):
             for s in range(ns):
-                near(functools.partial(settle, s, role=role))
+                if role in roles_of(s):
+                    late_here = True if role == OWN or s == ns - 1 else middle
+
+                    @pl.when(late_here)
+                    def _():
+                        near(functools.partial(settle, s, role=role))
 
     def settle_at(s, k):
         def both(zk):
-            for role in (OTHER, OWN):
+            for role in roles_of(s):
                 settle(s, zk, role)
 
         around(k, both)
@@ -621,11 +658,11 @@
             relay(nc + s, k)
 
             def make(zk, s=s):
-                for role in (OTHER, OWN):
+                for role in roles_of(s):
                     produce(s, zk, role)
 
             def join(zk, s=s):
-                for role in (OTHER, OWN):
+                for role in roles_of(s):
                     combine(s, zk, role)
 
             around(k, make)
@@ -634,6 +671,10 @@
                 @pl.when(k == 3)
                 def _():
                     settle_near()
+            else:
+                @pl.when((k == 2) & ends)
+                def _():
+                    near(functools.partial(settle, s - 1, role=OTHER))
 
             @pl.when(k > 2)
             def _():
@@ -737,6 +778,12 @@
     def per_piece(*lead):
         return [pltpu.VMEM((*lead, local_len, size), bf16) for _, size in pieces]
 
+    def per_sum(*rest):
+        return [
+            pltpu.VMEM((nz, 1 if packed(size) else 2, *rest, local_len, size * (1 + packed(size))), bf16)
+            for _, size in pieces
+        ]
+
     mixed, keys, values = pl.pallas_call(
         functools.partial(kernel, n_dp, n_mp, pieces),
         out_shape=(
@@ -744,7 +791,7 @@
             pltpu.VMEM((maxlen, kw), bf16),
             pltpu.VMEM((maxlen, kw), bf16),
         ),
-        in_specs=[pl.BlockSpec(memory_space=pltpu.SMEM)] + [anywhere] * 9,
+        in_specs=[anywhere] * 10,
         out_specs=(pl.BlockSpec(memory_space=pltpu.VMEM),) * 3,
         scratch_shapes=[
             pltpu.VMEM((local_len, width), bf16),
@@ -769,12 +816,13 @@
             pltpu.VMEM((2, maxlen, kw), bf16),
             pltpu.VMEM((2, maxlen, kw), bf16),
             pltpu.VMEM((2, maxlen, kw), bf16),
-            *per_piece(nz, 2, 2, pairs),
-            *per_piece(nz, 2, pairs),
-            *per_piece(nz, 2, far),
+            pltpu.SMEM((1,), jnp.int32),
+            *per_sum(2, pairs),
+            *per_sum(pairs),
+            *per_sum(far),
             *per_piece(nz),
             *per_piece(2, nz),
-            dma((nc + 6,)),
+            dma((nc + 7,)),
             dma((2, 2, nz)),
             dma((nc + ns, nz)),
             dma((1,)),

time: 124 us -> 123 us (level)
  no operation moved by 1% of the time
where the time goes in v4:
time: 123 us
  Pallas kernels  119 us (97%)
  local copies, waits for them, and re-layouts  2.42 us (2%)
  between operations  1.29 us (1%)
    pallas_call x1, Pallas kernels, local(): pl.pallas_call(functools.partial(kernel, n_dp, n_mp, pieces), out_shape=(...  119 us

profile of v4, /device:TPU:0, one launch (start us, length us, event | category | flops | bytes accessed | tf_op | source)
XLA Modules:
  0.0 123.1 jit_solution(10884206482892142964)
XLA Ops:
  1.3 119.4 %shard_map.121 = (bf16[128,4608]{1,0:T(8,128)(2,1)S(1)}, bf16[512,256]{1,0:T(8,128)(2,1)S(1)}, bf16[512,256]{1,0:T(8,128)(2,1)S(1)}) custom-call(s32[1]{0:T(128)S(6)} %copy.19.len_in, bf16[128,4608]{1,0:T(8,128)(2,1)} %bitcast.10, f32[36,128]{1,0:T(8,128)} %bitcast.12, bf16[576,512]{1,0:T(8,128)(2,1)} %wq.1, bf16[576,256]{1,0:T(8,128)(2,1)} %wk.1, ...), custom_call_target="tpu_custom_call" | custom-call | tf_op jit(solution)/shard_map/pallas_call | solution.py:787
  120.7 1.0 copy.16
  121.7 0.7 copy.17
  122.4 0.7 copy.18

commit v5 on v4

--- a/solution.py
+++ b/solution.py
@@ -633,8 +633,9 @@
         share(j, 1 - x).wait_recv()
     for s in range(ns):
         near(functools.partial(produce, s, role=OTHER))
-    for s in range(ns):
-        near(functools.partial(combine, s, role=OTHER))
+        if s > 0:
+            near(functools.partial(combine, s - 1, role=OTHER))
+    near(functools.partial(combine, ns - 1, role=OTHER))
 
     def settle_near():
         for role in (OTHER, OWN):

time: 123 us -> 123 us (level)
  no operation moved by 1% of the time
where the time goes in v5:
time: 123 us
  Pallas kernels  119 us (97%)
  local copies, waits for them, and re-layouts  2.42 us (2%)
  between operations  1.29 us (1%)
    pallas_call x1, Pallas kernels, local(): pl.pallas_call(functools.partial(kernel, n_dp, n_mp, pieces), out_shape=(...  119 us

profile of v5, /device:TPU:0, one launch (start us, length us, event | category | flops | bytes accessed | tf_op | source)
XLA Modules:
  0.0 122.7 jit_solution(13569755098823654692)
XLA Ops:
  1.3 119.0 %shard_map.121 = (bf16[128,4608]{1,0:T(8,128)(2,1)S(1)}, bf16[512,256]{1,0:T(8,128)(2,1)S(1)}, bf16[512,256]{1,0:T(8,128)(2,1)S(1)}) custom-call(s32[1]{0:T(128)S(6)} %copy.19.len_in, bf16[128,4608]{1,0:T(8,128)(2,1)} %bitcast.10, f32[36,128]{1,0:T(8,128)} %bitcast.12, bf16[576,512]{1,0:T(8,128)(2,1)} %wq.1, bf16[576,256]{1,0:T(8,128)(2,1)} %wk.1, ...), custom_call_target="tpu_custom_call" | custom-call | tf_op jit(solution)/shard_map/pallas_call | solution.py:788
  120.3 1.0 copy.16
  121.3 0.7 copy.17
  122.0 0.7 copy.18
